TPU v7x, 32 devices: a whole 2x2x4 slice. The times are simulated.
32 devices in a mesh: cp: 4 (over z), fsdp: 8 (over y, x, core).
Axes of the slice: x: 2, y: 2, z: 4, core: 2. Of those that a mesh axis runs over, the one named last changes fastest.
Arguments:
- tokens: int32 [256, 256], P('fsdp', 'cp')
- lengths: int32 [256], P('fsdp')
- embed_table: bfloat16 [33, 480], replicated
- layer_vecs: float32 [9, 480], P(None, 'fsdp')
- w_qkv: bfloat16 [480, 3, 20, 24], P('fsdp')
- w_out: bfloat16 [480, 480], P('fsdp')
- w_up: bfloat16 [480, 1920], P('fsdp')
- b_up: float32 [1920], P('fsdp')
- w_down: bfloat16 [1920, 480], P('fsdp')
- grad_out: bfloat16 [256, 256, 480], P('fsdp', 'cp')
Outputs:
- output 1: bfloat16 [256, 256, 480], P('fsdp', 'cp')
- output 2: float32 [33, 480], replicated
- output 3: float32 [9, 480], P(None, 'fsdp')
- output 4: float32 [480, 3, 20, 24], P('fsdp')
- output 5: float32 [480, 480], P('fsdp')
- output 6: float32 [480, 1920], P('fsdp')
- output 7: float32 [1920], P('fsdp')
- output 8: float32 [1920, 480], P('fsdp')
All inputs are finite; a program needn't handle non-finite values.
Results may differ from a plain program's by a relative error of at most 0.0101958.
Values are sent between devices in bfloat16 or wider.
A program may use at most 1 GiB of HBM per device.

v0:
```python
import functools
import typing

import numpy as np
import jax
import jax.numpy as jnp
from jax import lax
from jax.experimental import pallas as pl
from jax.experimental.pallas import tpu as pltpu
from jax.sharding import PartitionSpec as P

MASK_ID = 32
LN_EPS = 1e-5
ROPE_BASE = 10000.0
TRAIN_RATIO = 0.15 * 0.8
NEG_BIG = -1e30
D = 480
INV_D = 1.0 / D
H = 20
HD = 24
HP = 32
QP = H * HP
NQKV = 2 * QP + D
F = 1920
S = 256
VP = 40
PIECES = 8
PV = D // PIECES
PR = 64
DX = PIECES * PR
FR = 256
FV = F // PIECES
SQRT_HALF = 0.7071067811865476
INV_SQRT_2PI = 0.3989422804014327
LANES = 128
HALF = 16
ROT = HD // 2
MIB = 2 ** 20
MESH = pl.DeviceIdType.MESH
QUARTERS = 4
GROUPS = H // QUARTERS

NN = (((1,), (0,)), ((), ()))
NT = (((1,), (1,)), ((), ()))


def dot(a, b, dims=NN):
    return lax.dot_general(a, b, dims, preferred_element_type=jnp.float32)


def eye(n):
    return (lax.broadcasted_iota(jnp.int32, (n, n), 0) == lax.broadcasted_iota(jnp.int32, (n, n), 1)).astype(jnp.float32).astype(jnp.bfloat16)


def fold(z):
    return z[:, :LANES] + z[:, LANES:]


def col_sum(z):
    return jnp.sum(z, axis=0, keepdims=True)


def chunks(total, width):
    return [slice(j, min(j + width, total)) for j in range(0, total, width)]


def zero(*refs):
    for ref in refs:
        ref[...] = jnp.zeros_like(ref)


def head(h, width=None):
    width = HP if width is None else width
    return slice(width * h, width * (h + 1))


def side_by_side(g, block):
    return jnp.concatenate([place(block(QUARTERS * g + slot), slot) for slot in range(QUARTERS)], axis=1)


def cols(ref):
    return [ref[:, j:j + 1] for j in range(6)]


def embed(tok, length, table_t):
    pos = lax.broadcasted_iota(jnp.int32, (1, S), 1)
    is_mask = tok == MASK_ID
    valid = pos < length
    n_mask = jnp.sum(is_mask.astype(jnp.float32), axis=1, keepdims=True)
    len_f = jnp.full((1, 1), length, jnp.int32).astype(jnp.float32)
    scale = (1.0 - TRAIN_RATIO) / (1.0 - n_mask / len_f)
    keep = jnp.where(is_mask | jnp.logical_not(valid), 0.0, scale)
    one_hot = (lax.broadcasted_iota(jnp.int32, (VP, S), 0) == tok).astype(jnp.float32).astype(jnp.bfloat16)
    return dot(table_t, one_hot) * keep, keep, one_hot, valid


def norm_stats(z):
    mean = col_sum(z) * INV_D
    cen = z - mean
    var = col_sum(cen * cen) * INV_D
    rstd = lax.rsqrt(var + LN_EPS)
    return cen * rstd, rstd


def norm_back(d_out, gain, xhat, rstd):
    d_hat = d_out * gain
    m1 = col_sum(d_hat) * INV_D
    m2 = col_sum(d_hat * xhat) * INV_D
    return rstd * (d_hat - m1 - xhat * m2)


def spread(z, src, dst):
    src[...] = z
    for j in range(PIECES):
        dst[PR * j:PR * j + PV, :] = src[PV * j:PV * (j + 1), :]
    return dst[...]


def pack(z, src, dst):
    src[...] = z
    for j in range(PIECES):
        dst[PV * j:PV * (j + 1), :] = src[PR * j:PR * j + PV, :]
    return dst[...]


def split3(z):
    parts = []
    for _ in range(3):
        parts.append(z.astype(jnp.bfloat16))
        z = z - parts[-1].astype(jnp.float32)
    return parts


def lane_sums(acc):
    ones = jnp.ones((8, LANES), jnp.bfloat16)
    hi, mid, lo = (dot(ones, part, NT)[:1] for part in split3(acc))
    return hi + (mid + lo)


def minus_rows(block, first, value):
    row = lax.broadcasted_iota(jnp.int32, block.shape, 0)
    for n, part in enumerate(split3(-value)):
        block = jnp.where(row == first + n, part.astype(jnp.float32), block)
    return block.astype(jnp.bfloat16)


def flip(w_ref, out, width):
    ident = eye(LANES)
    for sl in chunks(width, LANES):
        n = sl.stop - sl.start
        out[sl, :] = dot(ident[:n, :n], w_ref[:, sl], NT).astype(jnp.bfloat16)


def place(rows, slot):
    parts = []
    if slot:
        parts.append(jnp.zeros((HP * slot, S), rows.dtype))
    parts.append(rows)
    if slot < 3:
        parts.append(jnp.zeros((HP * (3 - slot), S), rows.dtype))
    return jnp.concatenate(parts, axis=0)


def rope_store(lin, out, base, ca, cb, sn):
    for h in range(H):
        lo, up = lin[HP * h:HP * h + HALF], lin[HP * h + HALF:HP * (h + 1)]
        out[0, base + HP * h:base + HP * h + HALF, :] = (lo * ca - up * sn).astype(jnp.bfloat16)
        out[0, base + HP * h + HALF:base + HP * (h + 1), :] = (up * cb + lo * sn).astype(jnp.bfloat16)


def attn_fwd_kernel(len_ref, tok_ref, table_ref, vec_ref, bias_ref, rope_ref, w_ref, wo_loc, wu_loc, wd_loc, g_loc, g_part,
                    q_out, k_out, krow_out, vrow_out, o_out, lse_out, wo_all, wu_all, wd_all, g_all,
                    wt, v_t, sp, sx, w_send, w_recv, g_send, g_recv, loc_sem):
    step = pl.program_id(0)
    last = pl.num_programs(0) - 1
    f, c = lax.axis_index('fsdp'), lax.axis_index('cp')
    pairs = [(wo_loc, wo_all), (wu_loc, wu_all), (wd_loc, wd_all)]
    g_puts, g_near = grad_puts(g_loc, g_all, pl.ds(EARLY, g_loc.shape[1] - EARLY), (g_send, g_recv), loc_sem.at[len(pairs)], c)
    w_puts = [copy_to(loc, full.at[f], (w_send.at[m], w_recv.at[m]), k, {'fsdp': f ^ k}) for m, (loc, full) in enumerate(pairs) for k in OWN_PUTS]
    w_fwds = [copy_to(full.at[f ^ k], full.at[f ^ k], (w_send.at[m], w_recv.at[m]), k + 1, {'fsdp': f ^ 1}) for m, (_, full) in enumerate(pairs) for k in FAR]
    local = [pltpu.make_async_copy(loc, full.at[f], loc_sem.at[m]) for m, (loc, full) in enumerate(pairs)]
    local.append(g_near)

    @pl.when(step == 0)
    def _():
        enter([{'fsdp': f ^ k} for k in OWN_PUTS] + [{'cp': (c + d) % QUARTERS} for d in range(1, QUARTERS)])
        for copy in w_puts + g_puts + local:
            copy.start()
        zero(sx)
        flip(w_ref, wt, NQKV)

    @pl.when(step == last - 1)
    def _():
        for m in range(len(pairs)):
            for n, k in enumerate(OWN_PUTS):
                if k in FAR:
                    w_puts[m * len(OWN_PUTS) + n].wait_recv()
        for copy in w_fwds:
            copy.start()

    e_t, _, _, valid = embed(tok_ref[0], len_ref[step], table_ref[...])
    xhat, _ = norm_stats(e_t)
    g1, c1, _, _, _, _ = cols(vec_ref)
    h_t = spread(xhat * g1 + c1, sp, sx).astype(jnp.bfloat16)
    mask_row = jnp.where(valid, 0.0, NEG_BIG)
    cos_q, cos_q2, sin_q, cos_k, sin_k, cos_k2 = (rope_ref[r] for r in range(6))
    cos_k2 = jnp.where(lax.broadcasted_iota(jnp.int32, (HALF, S), 0) == HALF - 1, mask_row, cos_k2)
    rope_store(dot(wt[:QP, :], h_t) + bias_ref[:QP, :], q_out, 0, cos_q, cos_q2, sin_q)
    rope_store(dot(wt[QP:2 * QP, :], h_t) + bias_ref[QP:2 * QP, :], k_out, 0, cos_k, cos_k2, sin_k)
    v_lin = dot(wt[2 * QP:, :], h_t) + bias_ref[2 * QP:, :]
    pad = (lax.broadcasted_iota(jnp.int32, (HP - HD, S), 0) < 3).astype(jnp.float32)
    for h in range(H):
        v_t[head(h), :] = jnp.concatenate([v_lin[head(h, HD)], pad], axis=0).astype(jnp.bfloat16)
    ident = eye(S)
    krow_out[0] = dot(ident, k_out[0], NT).astype(jnp.bfloat16)
    vrow_out[0] = dot(ident, v_t[...], NT).astype(jnp.bfloat16)
    def scores(g):
        return dot(krow_out[0, :, head(g, LANES)], side_by_side(g, lambda h: q_out[0, head(h), :]))

    def finish(h, top, tot, p):
        o_h = dot(v_t[head(h), :], p)
        o_out[0, head(h, HD), :] = o_h[:HD] / tot
        lse_out[0, h:h + 1, :] = top + jnp.log(tot)

    pending = None
    ahead = scores(0)
    for g in range(GROUPS):
        now = ahead
        if g + 1 < GROUPS:
            ahead = scores(g + 1)
        for slot in range(QUARTERS):
            sc = now[:, head(slot, S)]
            top = jnp.max(sc, axis=0, keepdims=True)
            p = jnp.exp(sc - top)
            if pending:
                finish(*pending)
            pending = (QUARTERS * g + slot, top, col_sum(p), p.astype(jnp.bfloat16))
    finish(*pending)

    @pl.when(step == last)
    def _():
        for n, copy in enumerate(w_puts):
            if OWN_PUTS[n % len(OWN_PUTS)] not in FAR:
                copy.wait_recv()
        for copy in w_fwds + g_puts:
            copy.wait_recv()
        for copy in local:
            copy.wait()
        for copy in w_puts + w_fwds + g_puts:
            copy.wait_send()


def ffn_kernel(len_ref, tok_ref, table_ref, vec_ref, bup_ref, o_ref, g_ref, wo_ref, wu_ref, wd_ref,
               dres_ref, dwd_ref, dwu_ref, sv_ref, out_all, wot, wut, wdt, gelu_s, dup_s, dbup_ref, dvec_ref, sp, sx, sy, obuf, o_send, o_recv, loc_sem):
    step = pl.program_id(0)
    n_step = pl.num_programs(0)
    c = lax.axis_index('cp')
    rows = S // QUARTERS

    def out_puts(i):
        slot = lax.rem(i, 2)
        part = lambda p: obuf.at[slot, pl.ds(pl.multiple_of(p * rows, rows), rows)]
        dst = out_all.at[c * n_step + i]
        far = [copy_to(part((c + d) % QUARTERS), dst, (o_send.at[i], o_recv.at[i]), d, {'cp': (c + d) % QUARTERS}) for d in NEAR_CP]
        return far, pltpu.make_async_copy(part(c), dst, loc_sem.at[i])

    @pl.when(step == 0)
    def _():
        enter([{'cp': (c + d) % QUARTERS} for d in range(1, QUARTERS)])
        zero(sx, dwd_ref, dwu_ref, dbup_ref, dvec_ref)
        flip(wo_ref, wot, D)
        flip(wd_ref, wdt, D)
        flip(wu_ref, wut, F)

    @pl.when(step >= 2)
    def _():
        far, near = out_puts(step - 2)
        near.wait()
        for copy in far:
            copy.wait_send()

    _, _, b_o, gain2, bias2, b_down = cols(vec_ref)
    e_t, _, _, _ = embed(tok_ref[0], len_ref[step], table_ref[...])
    o_x = spread(o_ref[0], sp, sx).astype(jnp.bfloat16)
    x1 = e_t + dot(wot[...], o_x) + b_o
    xhat, rstd = norm_stats(x1)
    n_t = spread(xhat * gain2 + bias2, sp, sx).astype(jnp.bfloat16)
    g_t32 = dot(eye(D), g_ref[...].reshape(S, D), NT)
    g_t = g_t32.astype(jnp.bfloat16)
    for sl in chunks(F, D):
        up = dot(wut[sl, :], n_t) + bup_ref[sl, :]
        d_gelu = dot(wd_ref[sl, :], g_t)
        cdf = 0.5 * (1.0 + lax.erf(up * SQRT_HALF))
        pdf = jnp.exp(up * up * -0.5) * INV_SQRT_2PI
        gelu_s[sl, :] = (up * cdf).astype(jnp.bfloat16)
        d_up = d_gelu * (cdf + up * pdf)
        dup_s[sl, :] = d_up.astype(jnp.bfloat16)
        dbup_ref[sl, :] += fold(d_up)
    out_t = (x1 + dot(wdt[...], gelu_s[...]) + b_down).astype(jnp.bfloat16)
    obuf[lax.rem(step, 2)] = dot(eye(S), out_t, NT).astype(jnp.bfloat16)
    for j in range(PIECES):
        dwd_ref[j, :FV, :] += dot(gelu_s[head(j, FV), :], g_t, NT)
    for sl in chunks(F, 3 * LANES):
        dwu_ref[:, sl] += dot(n_t, dup_s[sl, :], NT)
    d_n = pack(dot(wu_ref[...], dup_s[...]), sy, sp)
    d_res = g_t32 + norm_back(d_n, gain2, xhat, rstd)
    dres_ref[0] = d_res
    for r, z in enumerate((d_res, d_n * xhat, d_n, g_t32)):
        dvec_ref[r] += fold(z)
    far, near = out_puts(step)
    for copy in far + [near]:
        copy.start()

    @pl.when(step == n_step - 1)
    def _():
        for r in range(4):
            sv_ref[r:r + 1, :] = lane_sums(dbup_ref[head(r, D), :])
            sv_ref[r + 4:r + 5, :] = lane_sums(dvec_ref[r])
        for back in range(2):
            far, near = out_puts(step - back)
            near.wait()
            for copy in far:
                copy.wait_send()

        def drain(i, carry):
            for copy in out_puts(i)[0]:
                copy.wait_recv()
            return carry

        lax.fori_loop(0, n_step, drain, 0)


def attn_bwd_kernel(len_ref, tok_ref, table_ref, vec_ref, rope_ref, q_ref, k_ref, krow_ref, vrow_ref, o_ref, lse_ref, dres_ref, wo_ref, w_ref, sv_in, dwd_src, dwu_src,
                    dwo_ref, dw_ref, sv_ref, pd_ref, pu_ref, da_s, dq_s, dk_s, dlin_s, dcmp_s, dlinb_s, dbias_ref, dvec_ref, dtab_ref, sp, sx, sy, *comm):
    step = pl.program_id(0)
    f, c = lax.axis_index('fsdp'), lax.axis_index('cp')
    refs = list(comm)
    b_send, b_recv, loc_sem = refs[-3:]
    outs = [(dwd_src, pd_ref, sl) for sl in FFN_SPLITS[0]] + [(dwu_src, pu_ref, sl) for sl in FFN_SPLITS[1]]
    units = [Unit(src, sl, *refs[m:-3:len(outs)], b_send.at[m], b_recv.at[m], loc_sem.at[m]) for m, (src, _, sl) in enumerate(outs)]

    def advance(*todo):
        for m, stage in todo:
            settle(units[m], stage, f, c)
        for m, stage in todo:
            for copy in stage_copies(units[m], stage, f, c):
                copy.start()

    def comm_point(late):
        for i in range(H // 2):
            point = 2 * i + late
            todo = [(m, stage) for m in range(len(units)) for stage, at in enumerate(POINTS) if stage and at + 3 * m == point]
            if todo:
                pl.when(step == i)(functools.partial(advance, *todo))

    @pl.when(step == 0)
    def _():
        enter(reduce_peers(f, c))
        for u in units:
            for copy in loads(u, f):
                copy.start()
        advance(*((m, 0) for m in range(len(units))))
        zero(sx, dwo_ref, dw_ref, dtab_ref, dbias_ref, dvec_ref)

    comm_point(0)

    d_res = dres_ref[0]
    d_res_b = d_res.astype(jnp.bfloat16)
    dwo_ref[...] += dot(spread(o_ref[0], sp, sx).astype(jnp.bfloat16), d_res_b, NT)
    d_attn = pack(dot(wo_ref[...], d_res_b), sy, sp)
    prod = d_attn * o_ref[0]
    pad = jnp.zeros((HP - HD, S), jnp.float32)
    for h in range(H):
        delta = col_sum(prod[head(h, HD)])
        da_s[head(h), :] = jnp.concatenate([d_attn[head(h, HD)], minus_rows(pad, 0, delta).astype(jnp.float32)], axis=0).astype(jnp.bfloat16)
    def q_block(h):
        q_h = q_ref[0, head(h), :]
        q_up = minus_rows(q_h[HALF:].astype(jnp.float32), ROT, lse_ref[0, h:h + 1, :])
        return jnp.concatenate([q_h[:HALF], q_up], axis=0)

    def scores(g):
        lanes = head(g, LANES)
        return dot(krow_ref[0, :, lanes], side_by_side(g, q_block)), dot(vrow_ref[0, :, lanes], side_by_side(g, lambda h: da_s[head(h), :]))

    def finish(h, p, ds):
        rows = head(h)
        dq_s[rows, :] = dot(k_ref[0, rows, :], ds)
        dk_s[rows, :] = dot(q_ref[0, rows, :], ds, NT)
        d_v = dot(da_s[rows, :], p, NT)[:HD]
        dlin_s[2 * QP + HD * h:2 * QP + HD * (h + 1), :] = d_v
        dcmp_s[2 * D + HD * h:2 * D + HD * (h + 1), :] = d_v

    pending = None
    ahead = scores(0)
    for g in range(GROUPS):
        now = ahead
        if g + 1 < GROUPS:
            ahead = scores(g + 1)
        for slot in range(QUARTERS):
            sc, d_p = (z[:, head(slot, S)] for z in now)
            p = jnp.exp(sc)
            ds = (p * d_p).astype(jnp.bfloat16)
            if pending:
                finish(*pending)
            pending = (QUARTERS * g + slot, p.astype(jnp.bfloat16), ds)
    finish(*pending)
    comm_point(1)
    cos_q, _, sin_q, cos_k, sin_k = (rope_ref[r] for r in range(5))
    for m, (src, cs, sn) in enumerate(((dq_s, cos_q, sin_q), (dk_s, cos_k, sin_k))):
        for h in range(H):
            lo, up = src[HP * h:HP * h + HALF, :], src[HP * h + HALF:HP * (h + 1), :]
            for n, z in enumerate((lo * cs + up * sn, up * cs - lo * sn)):
                wide, slim = QP * m + HP * h + HALF * n, D * m + HD * h + ROT * n
                dlin_s[wide:wide + HALF, :] = z
                dcmp_s[slim:slim + ROT, :] = z[:ROT]
    d_cmp = dcmp_s[...]
    dbias_ref[...] += fold(d_cmp)
    dcmp_b = d_cmp.astype(jnp.bfloat16)
    dlinb_s[...] = dlin_s[...].astype(jnp.bfloat16)
    e_t, keep, one_hot, _ = embed(tok_ref[0], len_ref[step], table_ref[...])
    xhat, rstd = norm_stats(e_t)
    g1, c1, _, _, _, _ = cols(vec_ref)
    h_t = spread(xhat * g1 + c1, sp, sx).astype(jnp.bfloat16)
    for sl in chunks(3 * D, 3 * LANES):
        dw_ref[:, sl] += dot(h_t, dcmp_b[sl, :], NT)
    d_h = pack(dot(w_ref[...], dlinb_s[...]), sy, sp)
    d_e = (norm_back(d_h, g1, xhat, rstd) + d_res) * keep
    dtab_ref[...] += dot(one_hot, d_e.astype(jnp.bfloat16), NT)
    dvec_ref[0] += fold(d_h * xhat)
    dvec_ref[1] += fold(d_h)

    @pl.when(step == pl.num_programs(0) - 1)
    def _():
        zero(sv_ref)
        sv_ref[:8, :] = sv_in[...]
        for r in range(5):
            sums = dvec_ref[r] if r < 2 else dbias_ref[head(r - 2, D), :]
            sv_ref[8 + r:9 + r, :] = lane_sums(sums)
        sv_ref[HALF:, :] = dtab_ref[...]
        for u, (_, out, sl) in zip(units, outs):
            settle(u, STAGES, f, c)
            out[:, sl] = u.fin[:out.shape[0], :]
            for stage in range(STAGES):
                for copy in stage_copies(u, stage, f, c):
                    copy.wait_send()


def enter(peers):
    barrier = pltpu.get_barrier_semaphore()
    for peer in peers:
        pl.semaphore_signal(barrier, inc=1, device_id=peer, device_id_type=MESH)
    pl.semaphore_wait(barrier, len(peers))


def copy_to(src, dst, sems, k, peer):
    return pltpu.make_async_remote_copy(src_ref=src, dst_ref=dst, send_sem=sems[0].at[k], recv_sem=sems[1].at[k], device_id=peer, device_id_type=MESH)


OWN_PUTS = (2, 4, 6, 1)
EARLY = 3
NEAR_CP = (2, 1, 3)
FAR = (2, 4, 6)


def grad_puts(src, dst, seqs, sems, loc, c):
    far = [copy_to(src.at[(c + d) % QUARTERS, seqs], dst.at[c, seqs], sems, d, {'cp': (c + d) % QUARTERS}) for d in NEAR_CP]
    return far, pltpu.make_async_copy(src.at[c, seqs], dst.at[c, seqs], loc)


def gather_kernel(w_ref, small_ref, tok_ref, g_ref, w_out, small_out, tok_out, g_out, w_send, w_recv, s_send, s_recv, t_send, t_recv, g_send, g_recv, loc_sem):
    f, c = lax.axis_index('fsdp'), lax.axis_index('cp')
    enter([{'fsdp': f ^ k} for k in range(1, PIECES)] + [{'cp': (c + d) % QUARTERS} for d in range(1, QUARTERS)])
    w_sems = (w_send, w_recv)
    smalls = [copy_to(small_ref, small_out.at[f], (s_send, s_recv), k, {'fsdp': f ^ k}) for k in range(1, PIECES)]
    smalls += [copy_to(tok_ref.at[(c + d) % QUARTERS], tok_out.at[c], (t_send, t_recv), d, {'cp': (c + d) % QUARTERS}) for d in range(1, QUARTERS)]
    puts = [copy_to(w_ref, w_out.at[f], w_sems, k, {'fsdp': f ^ k}) for k in OWN_PUTS]
    fwds = [copy_to(w_out.at[f ^ k], w_out.at[f ^ k], w_sems, k + 1, {'fsdp': f ^ 1}) for k in FAR]
    local = [pltpu.make_async_copy(a, b, loc_sem.at[m]) for m, (a, b) in enumerate(((w_ref, w_out.at[f]), (tok_ref.at[c], tok_out.at[c]), (small_ref, small_out.at[f])))]
    far, near = grad_puts(g_ref, g_out, pl.ds(0, EARLY), (g_send, g_recv), loc_sem.at[len(local)], c)
    local.append(near)
    for copy in puts + smalls + local + far:
        copy.start()
    for put, fwd in zip(puts, fwds):
        put.wait_recv()
        fwd.start()
    for copy in puts[len(FAR):] + smalls + fwds + far:
        copy.wait_recv()
    for copy in local:
        copy.wait()
    for copy in puts + smalls + fwds + far:
        copy.wait_send()


class Unit(typing.NamedTuple):
    src: typing.Any
    lanes: slice
    acc: typing.Any
    core: typing.Any
    xy: typing.Any
    xy2: typing.Any
    z: typing.Any
    fin: typing.Any
    send: typing.Any
    recv: typing.Any
    loc: typing.Any


STAGES = 5
POINTS = (0, 1, 3, 4, 6)
FFN_SPLITS = ((slice(0, 2 * LANES), slice(2 * LANES, D)), (slice(0, 8 * LANES), slice(8 * LANES, F)))


def reduce_peers(f, c):
    return [{'fsdp': f ^ k} for k in (1, 2, 4)] + [{'cp': (c + d) % QUARTERS} for d in range(1, QUARTERS)]


def loads(u, f):
    return [pltpu.make_async_copy(u.src.at[f ^ (2 * q), :, u.lanes], u.acc.at[q], u.loc.at[q]) for q in range(QUARTERS)]


def stage_copies(u, stage, f, c):
    rows = u.fin.shape[0]
    half, quarter = rows // 2, rows // QUARTERS
    lo, hi = pl.ds(0, half), pl.ds(half, half)
    own = lambda p: pl.ds(pl.multiple_of(p * quarter, 8), quarter)
    core, xp, yp = ({'fsdp': f ^ k} for k in (1, 2, 4))
    ac = u.acc
    if stage == 0:
        plan = [(u.src.at[(f ^ 1) ^ (2 * q), :, u.lanes], u.core.at[q], core) for q in (3, 1, 2, 0)]
    elif stage == 1:
        plan = [(ac.at[3, lo], u.xy.at[1], xp), (ac.at[3, hi], u.xy.at[3], yp), (ac.at[1, lo], u.xy.at[0], xp), (ac.at[2, hi], u.xy.at[2], yp)]
    elif stage == 2:
        plan = [(ac.at[2, lo], u.xy2.at[0], yp), (ac.at[1, hi], u.xy2.at[1], xp)]
    elif stage == 3:
        plan = [(ac.at[0, own((c + d) % QUARTERS)], u.z.at[d - 1], {'cp': (c + d) % QUARTERS}) for d in NEAR_CP]
    else:
        plan = [(u.fin.at[own(c)], u.fin.at[own(c)], {'cp': (c + d) % QUARTERS}) for d in NEAR_CP]
    return [copy_to(a, b, (u.send, u.recv), QUARTERS * stage + n, peer) for n, (a, b, peer) in enumerate(plan)]


def settle(u, stage, f, c):
    if not stage:
        return
    for copy in stage_copies(u, stage - 1, f, c):
        copy.wait_recv()
    rows = u.fin.shape[0]
    half, quarter = rows // 2, rows // QUARTERS
    lo, hi = slice(0, half), slice(half, rows)
    if stage == 1:
        for copy in loads(u, f):
            copy.wait()
        u.acc[...] += u.core[...]
    elif stage == 2:
        for q, part, n in ((2, lo, 1), (1, hi, 3), (0, lo, 0), (0, hi, 2)):
            u.acc[q, part] += u.xy[n]
    elif stage == 3:
        u.acc[0, lo] += u.xy2[0]
        u.acc[0, hi] += u.xy2[1]
    elif stage == QUARTERS:
        mine = pl.ds(pl.multiple_of(c * quarter, 8), quarter)
        u.fin[mine] = (u.acc[0, mine] + u.z[0]) + (u.z[1] + u.z[2])


def reduce_kernel(dw_src, dwo_src, small, d_qkv, d_out, small_out, buf, r_small, *refs):
    n_unit = len(SPLITS) + 1
    refs = list(refs)
    b_send, b_recv, m_send, m_recv, loc_sem = refs[-5:]
    refs = refs[:-5]
    f, c = lax.axis_index('fsdp'), lax.axis_index('cp')
    enter(reduce_peers(f, c))
    outs = [(dwo_src, d_out, slice(0, D))] + [(dw_src, d_qkv, sl) for sl in SPLITS]
    units = [Unit(src, sl, *refs[m::n_unit], b_send.at[m], b_recv.at[m], loc_sem.at[m]) for m, (src, _, sl) in enumerate(outs)]
    steps = [{'fsdp': f ^ k} for k in (1, 2, 4)] + [{'cp': c ^ 1}, {'cp': c ^ 2}]
    small_puts = [copy_to(buf.at[t], r_small.at[t], (m_send, m_recv), t, peer) for t, peer in enumerate(steps)]
    for u in units:
        for copy in loads(u, f):
            copy.start()
    for t in range(n_unit + STAGES):
        todo = [(m, t - m) for m in range(n_unit) if 0 <= t - m <= STAGES]
        for m, stage in todo:
            settle(units[m], stage, f, c)
            if stage == STAGES:
                _, out, sl = outs[m]
                out[:, sl] = units[m].fin[:PV, :]
        if t <= STAGES:
            if t:
                small_puts[t - 1].wait_recv()
            value = buf[t - 1] + r_small[t - 1] if t else small[...]
            if t < STAGES:
                buf[t] = value
            else:
                small_out[...] = value
        for m, stage in todo:
            if stage < STAGES:
                for copy in stage_copies(units[m], stage, f, c):
                    copy.start()
        if t < STAGES:
            small_puts[t].start()
    for copy in small_puts:
        copy.wait_send()
    for u in units:
        for stage in range(STAGES):
            for copy in stage_copies(u, stage, f, c):
                copy.wait_send()


def rope_tables():
    inv_freq = (1.0 / (ROPE_BASE ** (np.arange(0, HD, 2, dtype=np.float32) / np.float32(HD)))).astype(np.float32)
    angles = inv_freq[:, None] * np.arange(S, dtype=np.float32)[None, :]
    cos, sin = np.zeros((16, S), np.float32), np.zeros((16, S), np.float32)
    cos[:12], sin[:12] = np.cos(angles), np.sin(angles)
    scale = np.float32(HD ** -0.5)
    cos_q2 = cos * scale
    cos_q2[15] = 1.0
    cos_k2 = cos.copy()
    cos_k2[ROT:] = 1.0
    return np.stack([cos * scale, cos_q2, sin * scale, cos, sin, cos_k2])


def pad_heads(z):
    lead = z.shape[:-2]
    z = z.reshape(lead + (H, 2, HD // 2))
    z = jnp.pad(z, [(0, 0)] * len(lead) + [(0, 0), (0, 0), (0, 4)])
    return z.reshape(lead + (QP,))


def const(shape):
    return pl.BlockSpec(shape, lambda i, *_: (0,) * len(shape))


def per_seq(shape):
    return pl.BlockSpec((1,) + shape, lambda i, *_: (i,) + (0,) * len(shape))


def anys(n):
    return [pl.BlockSpec(memory_space=pl.ANY)] * n


def dma(*shape):
    return pltpu.SemaphoreType.DMA(shape)


def gather_all(w_loc, small, tok4, grad4):
    return pl.pallas_call(
        gather_kernel,
        in_specs=anys(4),
        out_specs=anys(4),
        out_shape=[b16(PIECES, *w_loc.shape), f32(PIECES, *small.shape), jax.ShapeDtypeStruct(tok4.shape, tok4.dtype), b16(*grad4.shape)],
        scratch_shapes=[dma(PIECES)] * 4 + [dma(QUARTERS)] * 5,
        compiler_params=pltpu.CompilerParams(collective_id=1, has_side_effects=True),
        name="gather_all",
    )(w_loc, small, tok4, grad4)


def unit_scratch(parts):
    v = lambda *shape: pltpu.VMEM(shape, jnp.float32)
    out = []
    for lead, div in ((4, 1), (4, 1), (4, 2), (2, 2), (3, 4)):
        out += [v(lead, r // div, n) for r, n in parts]
    return out + [v(r, n) for r, n in parts]


SPLITS = (slice(0, 6 * LANES), slice(6 * LANES, 3 * D))


def reduce_all(dw, dwo, small):
    vmem = pl.BlockSpec(memory_space=pltpu.VMEM)
    parts = [(PR, D)] + [(PR, sl.stop - sl.start) for sl in SPLITS]
    n = len(parts)
    scratch = [pltpu.VMEM((STAGES,) + small.shape, jnp.float32)] * 2 + unit_scratch(parts)
    scratch += [dma(n, QUARTERS * STAGES)] * 2 + [dma(STAGES)] * 2 + [dma(n, QUARTERS)]
    return pl.pallas_call(
        reduce_kernel,
        in_specs=anys(2) + [vmem],
        out_specs=[vmem] * 3,
        out_shape=[f32(PV, 3 * D), f32(PV, D), f32(*small.shape)],
        scratch_shapes=scratch,
        compiler_params=pltpu.CompilerParams(collective_id=2, has_side_effects=True, vmem_limit_bytes=58 * MIB),
        name="reduce_all",
    )(dw, dwo, small)


def call(kernel, cid, n, in_specs, out_specs, out_shape, scratch, flops, name, aliases={}):
    return pl.pallas_call(
        kernel,
        grid_spec=pltpu.PrefetchScalarGridSpec(num_scalar_prefetch=1, grid=(n,), in_specs=in_specs, out_specs=out_specs, scratch_shapes=scratch),
        out_shape=out_shape,
        compiler_params=pltpu.CompilerParams(dimension_semantics=("arbitrary",), vmem_limit_bytes=58 * MIB, collective_id=cid, has_side_effects=True),
        input_output_aliases=aliases,
        cost_estimate=pl.CostEstimate(flops=flops, bytes_accessed=20 * MIB, transcendentals=0),
        name=name,
    )


def f32(*shape):
    return jax.ShapeDtypeStruct(shape, jnp.float32)


def b16(*shape):
    return jax.ShapeDtypeStruct(shape, jnp.bfloat16)


def sv(*shape):
    return pltpu.VMEM(shape, jnp.float32)


def bv(*shape):
    return pltpu.VMEM(shape, jnp.bfloat16)


def solution(mesh):
    n_cp, n_fsdp = mesh.shape['cp'], mesh.shape['fsdp']

    def local_step(tokens, lengths, embed_table, layer_vecs, w_qkv, w_out, w_up, b_up, w_down, grad_out):
        n_seq, seq_loc = tokens.shape
        n = n_seq // n_cp
        cp_index, f_index = lax.axis_index('cp'), lax.axis_index('fsdp')
        rows_pad = lambda w: jnp.pad(w, ((0, PR - PV), (0, 0)))
        w_loc = jnp.concatenate([pad_heads(w_qkv[:, 0]), pad_heads(w_qkv[:, 1]), w_qkv[:, 2].reshape(PV, D)], axis=1)
        small = jnp.pad(jnp.concatenate([layer_vecs.reshape(-1), b_up]), (0, PIECES * LANES - 9 * PV - FV)).reshape(PIECES, LANES)
        grad4 = grad_out.reshape(n_cp, n, seq_loc, D)
        w_full, small, tok, grads = gather_all(rows_pad(w_loc), small, tokens.reshape(n_cp, n, seq_loc), grad4)
        w_full = w_full.reshape(DX, NQKV)
        small = small.reshape(n_fsdp, PIECES * LANES)
        vecs = small[:, :9 * PV].reshape(n_fsdp, 9, PV).transpose(1, 0, 2).reshape(9, D)
        bup = small[:, 9 * PV:9 * PV + FV].reshape(F, 1)
        tok = tok.transpose(1, 0, 2).reshape(n, 1, S)
        lens = lax.dynamic_slice(lengths, (cp_index * n,), (n,))
        table_t = jnp.pad(embed_table, ((0, VP - embed_table.shape[0]), (0, 0))).T
        vec_cols = jnp.concatenate([vecs[:2], vecs[5:], jnp.zeros((2, D), jnp.float32)], axis=0).T
        slot = np.arange(QP) % HP
        pad_one = jnp.asarray(np.stack([slot == HP - 1, slot >= HALF + ROT]).astype(np.float32))
        bias = jnp.concatenate([(pad_heads(vecs[2:4].reshape(2, H, HD)) + pad_one).reshape(2 * QP), vecs[4]])[:, None]
        rope = jnp.asarray(rope_tables())

        shared = [per_seq((1, S)), const((D, VP)), const((D, 8))]
        rope_spec = const(rope.shape)
        acts = [((QP, S), b16), ((QP, S), b16), ((S, QP), b16), ((S, QP), b16), ((D, S), f32), ((24, S), f32)]
        act_specs = [per_seq(shape) for shape, _ in acts]
        fwd = call(
            attn_fwd_kernel, 3, n,
            shared + [const((NQKV, 1)), rope_spec, const((DX, NQKV))] + anys(5),
            act_specs + anys(4),
            [kind(n, *shape) for shape, kind in acts] + [b16(PIECES, PR, D), b16(PIECES, PR, F), b16(PIECES, FV, D), b16(n_cp, n, seq_loc, D)],
            [bv(NQKV, DX), bv(QP, S), sv(D, S), sv(DX, S)] + [dma(3, PIECES)] * 2 + [dma(QUARTERS)] * 3,
            int(2e10), "attn_fwd", {11: 9})(lens, tok, table_t, vec_cols, bias, rope, w_full, rows_pad(w_out), rows_pad(w_up), w_down, grad4, grads)
        acts, (out_w, up_w, down_w, grads) = fwd[:6], fwd[6:]
        out_w, up_w, down_w = out_w.reshape(DX, D), up_w.reshape(DX, F), down_w.reshape(F, D)
        d_res, dwd, dwu, sv2, layer_out = call(
            ffn_kernel, 4, n,
            shared + [const((F, 1)), per_seq((D, S)), pl.BlockSpec((n_cp, 1, seq_loc, D), lambda i, *_: (0, i, 0, 0)), const((DX, D)), const((DX, F)), const((F, D))],
            [per_seq((D, S)), const((PIECES, FR, D)), const((DX, F)), const((8, D))] + anys(1),
            [f32(n, D, S), f32(PIECES, FR, D), f32(DX, F), f32(8, D), b16(n_seq, seq_loc, D)],
            [bv(D, DX), bv(F, DX), bv(D, F), bv(F, S), bv(F, S), sv(F, LANES), sv(4, D, LANES), sv(D, S), sv(DX, S), sv(DX, S), bv(2, S, D)]
            + [dma(n, QUARTERS)] * 2 + [dma(n)],
            int(4e10), "ffn")(lens, tok, table_t, vec_cols, bup, acts[4], grads, out_w, up_w, down_w)
        ffn_parts = [(r, sl.stop - sl.start) for r, splits in zip((FR, PR), FFN_SPLITS) for sl in splits]
        cut = lambda z: z.reshape(PIECES, PR, z.shape[1])
        dwo, dw, smalls, d_down_w, d_up_w = call(
            attn_bwd_kernel, 5, n,
            shared + [rope_spec] + act_specs + [per_seq((D, S)), const((DX, D)), const((DX, NQKV)), const((8, D))] + anys(2),
            [const((DX, D)), const((DX, 3 * D)), const((HALF + VP, D)), const((FV, D)), const((PV, F))],
            [f32(DX, D), f32(DX, 3 * D), f32(HALF + VP, D), f32(FV, D), f32(PV, F)],
            [bv(QP, S), sv(QP, S), sv(QP, S), sv(NQKV, S), sv(3 * D, S), bv(NQKV, S), sv(3 * D, LANES), sv(2, D, LANES), sv(VP, D), sv(D, S), sv(DX, S), sv(DX, S)]
            + unit_scratch(ffn_parts) + [dma(4, QUARTERS * STAGES)] * 2 + [dma(4, QUARTERS)],
            int(5e10), "attn_bwd")(lens, tok, table_t, vec_cols, rope, *acts, d_res, out_w, w_full, sv2, dwd, cut(dwu))
        d_qkv, d_out_w, smalls = reduce_all(cut(dw), cut(dwo), smalls)
        d_qkv = d_qkv.reshape((PV,) + w_qkv.shape[1:])
        all_vecs = jnp.concatenate([smalls[8:13], smalls[4:8]], axis=0)
        d_vecs = lax.dynamic_slice(all_vecs, (0, f_index * PV), (9, PV))
        d_bup = lax.dynamic_slice(smalls[:4].reshape(F), (f_index * FV,), (FV,))
        return layer_out, smalls[HALF:HALF + embed_table.shape[0]], d_vecs, d_qkv, d_out_w, d_up_w, d_bup, d_down_w

    rows = P('fsdp', None)
    in_specs = (P('fsdp', 'cp'), P('fsdp'), P(), P(None, 'fsdp'), P('fsdp', None, None, None), rows, rows, P('fsdp'), rows, P('fsdp', 'cp', None))
    out_specs = (P('fsdp', 'cp', None), P(), P(None, 'fsdp'), P('fsdp', None, None, None), rows, rows, P('fsdp'), rows)
    return jax.shard_map(local_step, mesh=mesh, in_specs=in_specs, out_specs=out_specs, check_vma=False)
```

profile of v0, /device:TPU:0, one launch (start us, length us, event | category | flops | bytes accessed | tf_op | source)
XLA Modules:
  0.0 284.0 jit_solution(15392760747729350143)
XLA Ops:
  0.7 1.1 fusion.7
  2.4 0.7 fusion.4.w_ref
  3.3 0.7 fusion.6.small_ref
  3.9 21.8 %gather_all.1 = (bf16[8,64,1760]{2,1,0:T(8,128)(2,1)}, f32[8,8,128]{2,1,0:T(8,128)}, s32[4,8,64]{2,1,0:T(8,128)}, bf16[4,8,64,480]{3,2,1,0:T(8,128)(2,1)}) custom-call(bf16[64,1760]{1,0:T(8,128)(2,1)} %fusion.4.w_ref, f32[8,128]{1,0:T(8,128)} %fusion.6.small_ref, s32[4,8,64]{2,1,0:T(8,128)} %bitcast.45, bf16[4,8,64,480]{3,2,1,0:T(8,128)(2,1)} %bitcast.27), custom_call_target="tpu_custom_call" | custom-call | tf_op jit(solution)/shard_map/gather_all/pallas_call | solution.py:644
  25.7 0.8 copy.64
  27.0 0.8 copy.55
  28.2 1.2 broadcast_in_dim.8.bias_ref
  29.4 0.7 copy.51
  30.1 0.7 reshape.92.tok_ref
  31.5 0.7 pad_bitcast_fusion.table_ref
  32.2 0.7 pad.38.wu_loc
  33.6 40.4 %attn_fwd.1 = (bf16[8,640,256]{2,1,0:T(8,128)(2,1)}, bf16[8,640,256]{2,1,0:T(8,128)(2,1)}, bf16[8,256,640]{2,1,0:T(8,128)(2,1)}, bf16[8,256,640]{2,1,0:T(8,128)(...) custom-call(s32[8]{0:T(128)} %dynamic_slice.9.len_ref, ...), custom_call_target="tpu_custom_call", output_to_operand_aliasing={{9}: (11, {})} | custom-call | flops 20000000000 | bytes 20971520 | tf_op jit(solution)/shard_map/attn_fwd/pallas_call | solution.py:740
  74.1 1.3 reshape.110.bup_ref
  75.4 63.5 %ffn.1 = (f32[8,480,256]{2,1,0:T(8,128)}, f32[8,256,480]{2,1,0:T(8,128)}, f32[512,1920]{1,0:T(8,128)}, f32[8,480]{1,0:T(8,128)}, bf16[32,64,480]{2,1,0:T(8,128)(2,1)}) custom-call(s32[8]{0:T(128)} %dynamic_slice.9.len_ref, s32[8,1,256]{2,1,0:T(1,128)} %reshape.92.tok_ref, bf16[480,40]{1,0:T(8,128)(2,1)} %pad_bitcast_fusion.table_ref, f32[480,8]{1,0:T(8,128)} %bitcast.37, ...), custom_call_target="tpu_custom_call" | custom-call | flops 40000000000 | bytes 20971520 | tf_op jit(solution)/shard_map/ffn/pallas_call | solution.py:749
  138.9 73.5 %attn_bwd.1 = (f32[512,480]{1,0:T(8,128)}, f32[512,1440]{1,0:T(8,128)}, f32[56,480]{1,0:T(8,128)}, f32[240,480]{1,0:T(8,128)}, f32[60,1920]{1,0:T(8,128)}) custom-call(s32[8]{0:T(128)} %dynamic_slice.9.len_ref, s32[8,1,256]{2,1,0:T(1,128)} %reshape.92.tok_ref, bf16[480,40]{1,0:T(8,128)(2,1)} %pad_bitcast_fusion.table_ref, f32[480,8]{1,0:T(8,128)} %bitcast.38, ...), custom_call_target="tpu_custom_call" | custom-call | flops 49999998976 | bytes 20971520 | tf_op jit(solution)/shard_map/attn_bwd/pallas_call | solution.py:759
  212.4 61.4 %reduce_all.1 = (f32[60,1440]{1,0:T(8,128)}, f32[60,480]{1,0:T(8,128)}, f32[56,480]{1,0:T(8,128)}) custom-call(f32[8,64,1440]{2,1,0:T(8,128)} %bitcast.26, f32[8,64,480]{2,1,0:T(8,128)} %bitcast.29, f32[56,480]{1,0:T(8,128)} %get-tuple-element.56.small), custom_call_target="tpu_custom_call" | custom-call | tf_op jit(solution)/shard_map/reduce_all/pallas_call | solution.py:672
  273.8 2.2 copy.59
  276.0 0.8 fusion.8
  276.8 0.7 slice.59
  277.5 0.7 fusion.5
  278.2 1.5 slice.58
  280.4 1.3 copy.70
  282.4 0.8 copy.72
  283.2 0.8 copy.73
  (57 shorter events, 4.3 us)
Async XLA Ops:
  0.6 2.5 copy-start.8
  0.6 2.6 copy-start.9
  1.8 26.1 %copy-start.7 = (f32[2,20,2,16]{3,2,1,0:T(2,128)S(1)}, f32[2,20,2,16]{3,2,1,0:T(2,128)}, u32[]{:S(2)}) copy-start(f32[2,20,2,16]{3,2,1,0:T(2,128)} %constant.53) | copy-start | bytes 15364
  2.1 28.7 %copy-start.10 = (s32[32]{0:T(128)S(1)}, s32[32]{0:T(128)}, u32[]{:S(2)}) copy-start(s32[32]{0:T(128)} %param.13) | copy-start | bytes 388
  2.1 29.2 %copy-start.6 = (bf16[33,480]{1,0:T(8,128)(2,1)S(1)}, bf16[33,480]{1,0:T(8,128)(2,1)}, u32[]{:S(2)}) copy-start(bf16[33,480]{1,0:T(8,128)(2,1)} %param.14) | copy-start | bytes 95044
  2.4 29.8 %copy-start.3 = (bf16[60,1920]{1,0:T(8,128)(2,1)S(1)}, bf16[60,1920]{1,0:T(8,128)(2,1)}, u32[]{:S(2)}) copy-start(bf16[60,1920]{1,0:T(8,128)(2,1)} %param.18) | copy-start | bytes 691204
  3.2 29.8 %copy-start.5 = (bf16[60,480]{1,0:T(8,128)(2,1)S(1)}, bf16[60,480]{1,0:T(8,128)(2,1)}, u32[]{:S(2)}) copy-start(bf16[60,480]{1,0:T(8,128)(2,1)} %param.17) | copy-start | bytes 172804
  212.4 68.0 %copy-start = (bf16[32,64,480]{2,1,0:T(8,128)(2,1)S(1)}, bf16[32,64,480]{2,1,0:T(8,128)(2,1)}, u32[]{:S(2)}) copy-start(bf16[32,64,480]{2,1,0:T(8,128)(2,1)} %get-tuple-element.85) | copy-start | bytes 5898244
  273.8 8.0 %copy-start.4 = (f32[60,480]{1,0:T(8,128)S(1)}, f32[60,480]{1,0:T(8,128)}, u32[]{:S(2)}) copy-start(f32[60,480]{1,0:T(8,128)} %get-tuple-element.89) | copy-start | bytes 345604
  276.0 6.4 %copy-start.2 = (f32[60,1920]{1,0:T(8,128)S(1)}, f32[60,1920]{1,0:T(8,128)}, u32[]{:S(2)}) copy-start(f32[60,1920]{1,0:T(8,128)} %get-tuple-element.90) | copy-start | bytes 1382404
  280.4 2.8 copy-start.1
where the time goes:
time: 284 us
  Pallas kernels  261 us (92%)
  local copies, waits for them, and re-layouts  20.3 us (7%)
    pallas_call x1, Pallas kernels, local_step(): call(attn_bwd_kernel, 5, n, shared + [rope_spec] + act_specs + [per_seq((...  73.5 us
    pallas_call x1, Pallas kernels, local_step(): call(ffn_kernel, 4, n, shared + [const((F, 1)), per_seq((D, S)), pl.Block...  63.5 us
    pallas_call x1, Pallas kernels, reduce_all(): pl.pallas_call(reduce_kernel, in_specs=anys(2) + [vmem], out_specs=[vmem]...  61.4 us
    pallas_call x1, Pallas kernels, local_step(): call(attn_fwd_kernel, 3, n, shared + [const((NQKV, 1)), rope_spec, const(...  40.4 us
    pallas_call x1, Pallas kernels, gather_all(): pl.pallas_call(gather_kernel, in_specs=anys(4), out_specs=anys(4), out_sh...  21.8 us

commit v1 on v0

--- a/solution.py
+++ b/solution.py
@@ -287,9 +287,16 @@
     n_t = spread(xhat * gain2 + bias2, sp, sx).astype(jnp.bfloat16)
     g_t32 = dot(eye(D), g_ref[...].reshape(S, D), NT)
     g_t = g_t32.astype(jnp.bfloat16)
-    for sl in chunks(F, D):
-        up = dot(wut[sl, :], n_t) + bup_ref[sl, :]
-        d_gelu = dot(wd_ref[sl, :], g_t)
+    def products(sl):
+        return dot(wut[sl, :], n_t), dot(wd_ref[sl, :], g_t)
+
+    parts = chunks(F, D)
+    ahead = products(parts[0])
+    for n, sl in enumerate(parts):
+        up, d_gelu = ahead
+        if n + 1 < len(parts):
+            ahead = products(parts[n + 1])
+        up = up + bup_ref[sl, :]
         cdf = 0.5 * (1.0 + lax.erf(up * SQRT_HALF))
         pdf = jnp.exp(up * up * -0.5) * INV_SQRT_2PI
         gelu_s[sl, :] = (up * cdf).astype(jnp.bfloat16)
@@ -298,18 +305,19 @@
         dbup_ref[sl, :] += fold(d_up)
     out_t = (x1 + dot(wdt[...], gelu_s[...]) + b_down).astype(jnp.bfloat16)
     obuf[lax.rem(step, 2)] = dot(eye(S), out_t, NT).astype(jnp.bfloat16)
+    d_down = dot(gelu_s[...], g_t, NT)
     for j in range(PIECES):
-        dwd_ref[j, :FV, :] += dot(gelu_s[head(j, FV), :], g_t, NT)
-    for sl in chunks(F, 3 * LANES):
+        dwd_ref[j, :FV, :] += d_down[head(j, FV)]
+    far, near = out_puts(step)
+    for copy in far + [near]:
+        copy.start()
+    for sl in chunks(F, 4 * LANES):
         dwu_ref[:, sl] += dot(n_t, dup_s[sl, :], NT)
     d_n = pack(dot(wu_ref[...], dup_s[...]), sy, sp)
     d_res = g_t32 + norm_back(d_n, gain2, xhat, rstd)
     dres_ref[0] = d_res
     for r, z in enumerate((d_res, d_n * xhat, d_n, g_t32)):
         dvec_ref[r] += fold(z)
-    far, near = out_puts(step)
-    for copy in far + [near]:
-        copy.start()
 
     @pl.when(step == n_step - 1)
     def _():
@@ -421,7 +429,7 @@
     xhat, rstd = norm_stats(e_t)
     g1, c1, _, _, _, _ = cols(vec_ref)
     h_t = spread(xhat * g1 + c1, sp, sx).astype(jnp.bfloat16)
-    for sl in chunks(3 * D, 3 * LANES):
+    for sl in chunks(3 * D, 4 * LANES):
         dw_ref[:, sl] += dot(h_t, dcmp_b[sl, :], NT)
     d_h = pack(dot(w_ref[...], dlinb_s[...]), sy, sp)
     d_e = (norm_back(d_h, g1, xhat, rstd) + d_res) * keep
@@ -549,7 +557,8 @@
     if stage == 1:
         for copy in loads(u, f):
             copy.wait()
-        u.acc[...] += u.core[...]
+        for q in (3, 1, 2, 0):
+            u.acc[q] += u.core[q]
     elif stage == 2:
         for q, part, n in ((2, lo, 1), (1, hi, 3), (0, lo, 0), (0, hi, 2)):
             u.acc[q, part] += u.xy[n]
@@ -575,27 +584,31 @@
     for u in units:
         for copy in loads(u, f):
             copy.start()
-    for t in range(n_unit + STAGES):
-        todo = [(m, t - m) for m in range(n_unit) if 0 <= t - m <= STAGES]
-        for m, stage in todo:
-            settle(units[m], stage, f, c)
-            if stage == STAGES:
-                _, out, sl = outs[m]
-                out[:, sl] = units[m].fin[:PV, :]
-        if t <= STAGES:
-            if t:
-                small_puts[t - 1].wait_recv()
-            value = buf[t - 1] + r_small[t - 1] if t else small[...]
+    order = sorted((2 * stage + m, stage, m) for m in range(n_unit) for stage in range(1, STAGES + 1))
+    for u in units:
+        for copy in stage_copies(u, 0, f, c):
+            copy.start()
+    buf[0] = small[...]
+    small_puts[0].start()
+    small_at = {order[n_unit * t - 1]: t for t in range(1, STAGES + 1)}
+    for op in order:
+        _, stage, m = op
+        settle(units[m], stage, f, c)
+        if stage < STAGES:
+            for copy in stage_copies(units[m], stage, f, c):
+                copy.start()
+        else:
+            _, out, sl = outs[m]
+            out[:, sl] = units[m].fin[:PV, :]
+        if op in small_at:
+            t = small_at[op]
+            small_puts[t - 1].wait_recv()
+            value = buf[t - 1] + r_small[t - 1]
             if t < STAGES:
                 buf[t] = value
+                small_puts[t].start()
             else:
                 small_out[...] = value
-        for m, stage in todo:
-            if stage < STAGES:
-                for copy in stage_copies(units[m], stage, f, c):
-                    copy.start()
-        if t < STAGES:
-            small_puts[t].start()
     for copy in small_puts:
         copy.wait_send()
     for u in units:

time: 284 us -> 276 us (0.972)
  Pallas kernels: 261 us -> 252 us
    pallas_call x1, Pallas kernels: 61.4 us -> 53.5 us  [reduce_all(): pl.pallas_call(reduce_kernel, in_specs=anys(2) + [vmem], out_specs=[vmem]...]
where the time goes in v1:
time: 276 us; the launch traced here: 275 us
  Pallas kernels  252 us (91%)
  local copies, waits for them, and re-layouts  20.3 us (7%)
    pallas_call x1, Pallas kernels, local_step(): call(attn_bwd_kernel, 5, n, shared + [rope_spec] + act_specs + [per_seq((...  74.1 us
    pallas_call x1, Pallas kernels, local_step(): call(ffn_kernel, 4, n, shared + [const((F, 1)), per_seq((D, S)), pl.Block...  62 us
    pallas_call x1, Pallas kernels, reduce_all(): pl.pallas_call(reduce_kernel, in_specs=anys(2) + [vmem], out_specs=[vmem]...  53.5 us
    pallas_call x1, Pallas kernels, local_step(): call(attn_fwd_kernel, 3, n, shared + [const((NQKV, 1)), rope_spec, const(...  40.4 us
    pallas_call x1, Pallas kernels, gather_all(): pl.pallas_call(gather_kernel, in_specs=anys(4), out_specs=anys(4), out_sh...  21.8 us

profile of v1, /device:TPU:0, one launch (start us, length us, event | category | flops | bytes accessed | tf_op | source)
XLA Modules:
  0.0 275.2 jit_solution(4118247341615215183)
XLA Ops:
  0.7 1.1 fusion.7
  2.4 0.7 fusion.4.w_ref
  3.3 0.7 fusion.6.small_ref
  3.9 21.8 %gather_all.1 = (bf16[8,64,1760]{2,1,0:T(8,128)(2,1)}, f32[8,8,128]{2,1,0:T(8,128)}, s32[4,8,64]{2,1,0:T(8,128)}, bf16[4,8,64,480]{3,2,1,0:T(8,128)(2,1)}) custom-call(bf16[64,1760]{1,0:T(8,128)(2,1)} %fusion.4.w_ref, f32[8,128]{1,0:T(8,128)} %fusion.6.small_ref, s32[4,8,64]{2,1,0:T(8,128)} %bitcast.45, bf16[4,8,64,480]{3,2,1,0:T(8,128)(2,1)} %bitcast.27), custom_call_target="tpu_custom_call" | custom-call | tf_op jit(solution)/shard_map/gather_all/pallas_call | solution.py:657
  25.7 0.8 copy.64
  27.0 0.8 copy.55
  28.2 1.2 broadcast_in_dim.8.bias_ref
  29.4 0.7 copy.51
  30.1 0.7 reshape.92.tok_ref
  31.5 0.7 pad_bitcast_fusion.table_ref
  32.2 0.7 pad.38.wu_loc
  33.6 40.4 %attn_fwd.1 = (bf16[8,640,256]{2,1,0:T(8,128)(2,1)}, bf16[8,640,256]{2,1,0:T(8,128)(2,1)}, bf16[8,256,640]{2,1,0:T(8,128)(2,1)}, bf16[8,256,640]{2,1,0:T(8,128)(...) custom-call(s32[8]{0:T(128)} %dynamic_slice.9.len_ref, ...), custom_call_target="tpu_custom_call", output_to_operand_aliasing={{9}: (11, {})} | custom-call | flops 20000000000 | bytes 20971520 | tf_op jit(solution)/shard_map/attn_fwd/pallas_call | solution.py:753
  74.1 1.3 reshape.110.bup_ref
  75.4 62.0 %ffn.1 = (f32[8,480,256]{2,1,0:T(8,128)}, f32[8,256,480]{2,1,0:T(8,128)}, f32[512,1920]{1,0:T(8,128)}, f32[8,480]{1,0:T(8,128)}, bf16[32,64,480]{2,1,0:T(8,128)(2,1)}) custom-call(s32[8]{0:T(128)} %dynamic_slice.9.len_ref, s32[8,1,256]{2,1,0:T(1,128)} %reshape.92.tok_ref, bf16[480,40]{1,0:T(8,128)(2,1)} %pad_bitcast_fusion.table_ref, f32[480,8]{1,0:T(8,128)} %bitcast.37, ...), custom_call_target="tpu_custom_call" | custom-call | flops 40000000000 | bytes 20971520 | tf_op jit(solution)/shard_map/ffn/pallas_call | solution.py:762
  137.4 74.1 %attn_bwd.1 = (f32[512,480]{1,0:T(8,128)}, f32[512,1440]{1,0:T(8,128)}, f32[56,480]{1,0:T(8,128)}, f32[240,480]{1,0:T(8,128)}, f32[60,1920]{1,0:T(8,128)}) custom-call(s32[8]{0:T(128)} %dynamic_slice.9.len_ref, s32[8,1,256]{2,1,0:T(1,128)} %reshape.92.tok_ref, bf16[480,40]{1,0:T(8,128)(2,1)} %pad_bitcast_fusion.table_ref, f32[480,8]{1,0:T(8,128)} %bitcast.38, ...), custom_call_target="tpu_custom_call" | custom-call | flops 49999998976 | bytes 20971520 | tf_op jit(solution)/shard_map/attn_bwd/pallas_call | solution.py:772
  211.5 53.5 %reduce_all.1 = (f32[60,1440]{1,0:T(8,128)}, f32[60,480]{1,0:T(8,128)}, f32[56,480]{1,0:T(8,128)}) custom-call(f32[8,64,1440]{2,1,0:T(8,128)} %bitcast.26, f32[8,64,480]{2,1,0:T(8,128)} %bitcast.29, f32[56,480]{1,0:T(8,128)} %get-tuple-element.56.small), custom_call_target="tpu_custom_call" | custom-call | tf_op jit(solution)/shard_map/reduce_all/pallas_call | solution.py:685
  265.0 2.2 copy.59
  267.2 0.8 fusion.8
  268.0 0.7 slice.59
  268.7 0.7 fusion.5
  269.4 1.5 slice.58
  271.6 1.3 copy.70
  273.6 0.8 copy.72
  274.4 0.8 copy.73
  (57 shorter events, 4.3 us)
Async XLA Ops:
  0.6 2.5 copy-start.8
  0.6 2.6 copy-start.9
  1.8 26.1 %copy-start.7 = (f32[2,20,2,16]{3,2,1,0:T(2,128)S(1)}, f32[2,20,2,16]{3,2,1,0:T(2,128)}, u32[]{:S(2)}) copy-start(f32[2,20,2,16]{3,2,1,0:T(2,128)} %constant.53) | copy-start | bytes 15364
  2.1 28.7 %copy-start.10 = (s32[32]{0:T(128)S(1)}, s32[32]{0:T(128)}, u32[]{:S(2)}) copy-start(s32[32]{0:T(128)} %param.13) | copy-start | bytes 388
  2.1 29.2 %copy-start.6 = (bf16[33,480]{1,0:T(8,128)(2,1)S(1)}, bf16[33,480]{1,0:T(8,128)(2,1)}, u32[]{:S(2)}) copy-start(bf16[33,480]{1,0:T(8,128)(2,1)} %param.14) | copy-start | bytes 95044
  2.4 29.8 %copy-start.3 = (bf16[60,1920]{1,0:T(8,128)(2,1)S(1)}, bf16[60,1920]{1,0:T(8,128)(2,1)}, u32[]{:S(2)}) copy-start(bf16[60,1920]{1,0:T(8,128)(2,1)} %param.18) | copy-start | bytes 691204
  3.2 29.8 %copy-start.5 = (bf16[60,480]{1,0:T(8,128)(2,1)S(1)}, bf16[60,480]{1,0:T(8,128)(2,1)}, u32[]{:S(2)}) copy-start(bf16[60,480]{1,0:T(8,128)(2,1)} %param.17) | copy-start | bytes 172804
  211.5 60.1 %copy-start = (bf16[32,64,480]{2,1,0:T(8,128)(2,1)S(1)}, bf16[32,64,480]{2,1,0:T(8,128)(2,1)}, u32[]{:S(2)}) copy-start(bf16[32,64,480]{2,1,0:T(8,128)(2,1)} %get-tuple-element.85) | copy-start | bytes 5898244
  265.0 8.0 %copy-start.4 = (f32[60,480]{1,0:T(8,128)S(1)}, f32[60,480]{1,0:T(8,128)}, u32[]{:S(2)}) copy-start(f32[60,480]{1,0:T(8,128)} %get-tuple-element.89) | copy-start | bytes 345604
  267.2 6.4 %copy-start.2 = (f32[60,1920]{1,0:T(8,128)S(1)}, f32[60,1920]{1,0:T(8,128)}, u32[]{:S(2)}) copy-start(f32[60,1920]{1,0:T(8,128)} %get-tuple-element.90) | copy-start | bytes 1382404
  271.6 2.8 %copy-start.1 = (f32[240,480]{1,0:T(8,128)S(1)}, f32[240,480]{1,0:T(8,128)}, u32[]{:S(2)}) copy-start(f32[240,480]{1,0:T(8,128)} %get-tuple-element.92) | copy-start | bytes 1382404

commit v2 on v1

--- a/solution.py
+++ b/solution.py
@@ -465,7 +465,7 @@
 
 
 OWN_PUTS = (2, 4, 6, 1)
-EARLY = 3
+EARLY = 2
 NEAR_CP = (2, 1, 3)
 FAR = (2, 4, 6)
 

time: 276 us -> 276 us (level)
  no operation moved by 1% of the time
where the time goes in v2:
time: 276 us; the launch traced here: 275 us
  Pallas kernels  252 us (91%)
  local copies, waits for them, and re-layouts  20.3 us (7%)
    pallas_call x1, Pallas kernels, local_step(): call(attn_bwd_kernel, 5, n, shared + [rope_spec] + act_specs + [per_seq((...  75.6 us
    pallas_call x1, Pallas kernels, local_step(): call(ffn_kernel, 4, n, shared + [const((F, 1)), per_seq((D, S)), pl.Block...  63.4 us
    pallas_call x1, Pallas kernels, reduce_all(): pl.pallas_call(reduce_kernel, in_specs=anys(2) + [vmem], out_specs=[vmem]...  54.3 us
    pallas_call x1, Pallas kernels, local_step(): call(attn_fwd_kernel, 3, n, shared + [const((NQKV, 1)), rope_spec, const(...  39.2 us
    pallas_call x1, Pallas kernels, gather_all(): pl.pallas_call(gather_kernel, in_specs=anys(4), out_specs=anys(4), out_sh...  19.7 us

profile of v2, /device:TPU:0, one launch (start us, length us, event | category | flops | bytes accessed | tf_op | source)
XLA Modules:
  0.0 275.5 jit_solution(4243308857041936173)
XLA Ops:
  0.7 1.1 fusion.7
  2.4 0.7 fusion.4.w_ref
  3.3 0.7 fusion.6.small_ref
  3.9 19.7 %gather_all.1 = (bf16[8,64,1760]{2,1,0:T(8,128)(2,1)}, f32[8,8,128]{2,1,0:T(8,128)}, s32[4,8,64]{2,1,0:T(8,128)}, bf16[4,8,64,480]{3,2,1,0:T(8,128)(2,1)}) custom-call(bf16[64,1760]{1,0:T(8,128)(2,1)} %fusion.4.w_ref, f32[8,128]{1,0:T(8,128)} %fusion.6.small_ref, s32[4,8,64]{2,1,0:T(8,128)} %bitcast.45, bf16[4,8,64,480]{3,2,1,0:T(8,128)(2,1)} %bitcast.27), custom_call_target="tpu_custom_call" | custom-call | tf_op jit(solution)/shard_map/gather_all/pallas_call | solution.py:657
  23.6 0.8 copy.64
  24.9 0.8 copy.55
  26.1 1.2 broadcast_in_dim.8.bias_ref
  27.3 0.7 copy.51
  28.0 0.7 reshape.92.tok_ref
  29.4 0.7 pad_bitcast_fusion.table_ref
  30.1 0.7 pad.38.wu_loc
  31.5 39.2 %attn_fwd.1 = (bf16[8,640,256]{2,1,0:T(8,128)(2,1)}, bf16[8,640,256]{2,1,0:T(8,128)(2,1)}, bf16[8,256,640]{2,1,0:T(8,128)(2,1)}, bf16[8,256,640]{2,1,0:T(8,128)(...) custom-call(s32[8]{0:T(128)} %dynamic_slice.9.len_ref, ...), custom_call_target="tpu_custom_call", output_to_operand_aliasing={{9}: (11, {})} | custom-call | flops 20000000000 | bytes 20971520 | tf_op jit(solution)/shard_map/attn_fwd/pallas_call | solution.py:753
  70.7 1.3 reshape.110.bup_ref
  72.0 63.4 %ffn.1 = (f32[8,480,256]{2,1,0:T(8,128)}, f32[8,256,480]{2,1,0:T(8,128)}, f32[512,1920]{1,0:T(8,128)}, f32[8,480]{1,0:T(8,128)}, bf16[32,64,480]{2,1,0:T(8,128)(2,1)}) custom-call(s32[8]{0:T(128)} %dynamic_slice.9.len_ref, s32[8,1,256]{2,1,0:T(1,128)} %reshape.92.tok_ref, bf16[480,40]{1,0:T(8,128)(2,1)} %pad_bitcast_fusion.table_ref, f32[480,8]{1,0:T(8,128)} %bitcast.37, ...), custom_call_target="tpu_custom_call" | custom-call | flops 40000000000 | bytes 20971520 | tf_op jit(solution)/shard_map/ffn/pallas_call | solution.py:762
  135.4 75.6 %attn_bwd.1 = (f32[512,480]{1,0:T(8,128)}, f32[512,1440]{1,0:T(8,128)}, f32[56,480]{1,0:T(8,128)}, f32[240,480]{1,0:T(8,128)}, f32[60,1920]{1,0:T(8,128)}) custom-call(s32[8]{0:T(128)} %dynamic_slice.9.len_ref, s32[8,1,256]{2,1,0:T(1,128)} %reshape.92.tok_ref, bf16[480,40]{1,0:T(8,128)(2,1)} %pad_bitcast_fusion.table_ref, f32[480,8]{1,0:T(8,128)} %bitcast.38, ...), custom_call_target="tpu_custom_call" | custom-call | flops 49999998976 | bytes 20971520 | tf_op jit(solution)/shard_map/attn_bwd/pallas_call | solution.py:772
  211.0 54.3 %reduce_all.1 = (f32[60,1440]{1,0:T(8,128)}, f32[60,480]{1,0:T(8,128)}, f32[56,480]{1,0:T(8,128)}) custom-call(f32[8,64,1440]{2,1,0:T(8,128)} %bitcast.26, f32[8,64,480]{2,1,0:T(8,128)} %bitcast.29, f32[56,480]{1,0:T(8,128)} %get-tuple-element.56.small), custom_call_target="tpu_custom_call" | custom-call | tf_op jit(solution)/shard_map/reduce_all/pallas_call | solution.py:685
  265.3 2.2 copy.59
  267.5 0.8 fusion.8
  268.3 0.7 slice.59
  269.0 0.7 fusion.5
  269.7 1.5 slice.58
  271.9 1.3 copy.70
  273.9 0.8 copy.72
  274.7 0.8 copy.73
  (57 shorter events, 4.3 us)
Async XLA Ops:
  0.6 2.5 copy-start.8
  0.6 2.6 copy-start.9
  1.8 23.9 %copy-start.7 = (f32[2,20,2,16]{3,2,1,0:T(2,128)S(1)}, f32[2,20,2,16]{3,2,1,0:T(2,128)}, u32[]{:S(2)}) copy-start(f32[2,20,2,16]{3,2,1,0:T(2,128)} %constant.53) | copy-start | bytes 15364
  2.1 26.6 %copy-start.10 = (s32[32]{0:T(128)S(1)}, s32[32]{0:T(128)}, u32[]{:S(2)}) copy-start(s32[32]{0:T(128)} %param.13) | copy-start | bytes 388
  2.1 27.1 %copy-start.6 = (bf16[33,480]{1,0:T(8,128)(2,1)S(1)}, bf16[33,480]{1,0:T(8,128)(2,1)}, u32[]{:S(2)}) copy-start(bf16[33,480]{1,0:T(8,128)(2,1)} %param.14) | copy-start | bytes 95044
  2.4 27.7 %copy-start.3 = (bf16[60,1920]{1,0:T(8,128)(2,1)S(1)}, bf16[60,1920]{1,0:T(8,128)(2,1)}, u32[]{:S(2)}) copy-start(bf16[60,1920]{1,0:T(8,128)(2,1)} %param.18) | copy-start | bytes 691204
  3.2 27.7 %copy-start.5 = (bf16[60,480]{1,0:T(8,128)(2,1)S(1)}, bf16[60,480]{1,0:T(8,128)(2,1)}, u32[]{:S(2)}) copy-start(bf16[60,480]{1,0:T(8,128)(2,1)} %param.17) | copy-start | bytes 172804
  211.0 61.0 %copy-start = (bf16[32,64,480]{2,1,0:T(8,128)(2,1)S(1)}, bf16[32,64,480]{2,1,0:T(8,128)(2,1)}, u32[]{:S(2)}) copy-start(bf16[32,64,480]{2,1,0:T(8,128)(2,1)} %get-tuple-element.85) | copy-start | bytes 5898244
  265.3 8.0 %copy-start.4 = (f32[60,480]{1,0:T(8,128)S(1)}, f32[60,480]{1,0:T(8,128)}, u32[]{:S(2)}) copy-start(f32[60,480]{1,0:T(8,128)} %get-tuple-element.89) | copy-start | bytes 345604
  267.5 6.4 %copy-start.2 = (f32[60,1920]{1,0:T(8,128)S(1)}, f32[60,1920]{1,0:T(8,128)}, u32[]{:S(2)}) copy-start(f32[60,1920]{1,0:T(8,128)} %get-tuple-element.90) | copy-start | bytes 1382404
  271.9 2.8 %copy-start.1 = (f32[240,480]{1,0:T(8,128)S(1)}, f32[240,480]{1,0:T(8,128)}, u32[]{:S(2)}) copy-start(f32[240,480]{1,0:T(8,128)} %get-tuple-element.92) | copy-start | bytes 1382404
